TPU v7x, 32 devices: a whole 2x2x4 slice. The times are simulated.
32 devices in a mesh: shard: 32 (over z, y, x, core).
Axes of the slice: x: 2, y: 2, z: 4, core: 2. Of those that a mesh axis runs over, the one named last changes fastest.
Arguments:
- tokens: bfloat16 [384, 197, 384], P('shard'), may hold values from -6 to 6
- cotangent: bfloat16 [384, 197, 384], P('shard'), may hold values from -6 to 6
- image_count: int32 [32], P('shard'), may hold values from 6 to 12, as said below
- attention_gain: bfloat16 [384], P('shard'), may hold values from 0.099609375 to 1.8984375
- attention_shift: bfloat16 [384], P('shard'), may hold values from -3 to 3
- input_weight: bfloat16 [384, 1152], P('shard'), may hold values from -0.3125 to 0.3125
- query_bias: bfloat16 [384], P('shard'), may hold values from -3 to 3
- value_bias: bfloat16 [384], P('shard'), may hold values from -3 to 3
- output_weight: bfloat16 [384, 384], P('shard'), may hold values from -1.25 to 1.25
- output_bias: bfloat16 [384], P('shard'), may hold values from -3 to 3
- feed_gain: bfloat16 [384], P('shard'), may hold values from 0.099609375 to 1.8984375
- feed_shift: bfloat16 [384], P('shard'), may hold values from -3 to 3
- up_weight: bfloat16 [384, 1536], P('shard'), may hold values from -0.3125 to 0.3125
- up_bias: bfloat16 [1536], P('shard'), may hold values from -3 to 3
- down_weight: bfloat16 [1536, 384], P('shard'), may hold values from -0.15625 to 0.15625
- down_bias: bfloat16 [384], P('shard'), may hold values from -3 to 3
Outputs:
- output: bfloat16 [384, 197, 384], P('shard')
- tokens_grad: bfloat16 [384, 197, 384], P('shard')
- attention_gain_grad: float32 [384], P('shard')
- attention_shift_grad: float32 [384], P('shard')
- input_weight_grad: float32 [384, 1152], P('shard')
- query_bias_grad: float32 [384], P('shard')
- value_bias_grad: float32 [384], P('shard')
- output_weight_grad: float32 [384, 384], P('shard')
- output_bias_grad: float32 [384], P('shard')
- feed_gain_grad: float32 [384], P('shard')
- feed_shift_grad: float32 [384], P('shard')
- up_weight_grad: float32 [384, 1536], P('shard')
- up_bias_grad: float32 [1536], P('shard')
- down_weight_grad: float32 [1536, 384], P('shard')
- down_bias_grad: float32 [384], P('shard')
Inputs may be any that keep to these rules, and one draw needn't show every extreme that they name: Device i holds images in its first image_count[i] of 12 slots (rows 12 * i onward of tokens); its other slots are empty. Some device holds 12 images and some 12 // 2.
All inputs are finite; a program needn't handle non-finite values.
Results may differ from a plain program's by a relative error of at most 0.013.
The roundings to bfloat16 on the way count: a program that leaves them out, or rounds other values in their place, can miss the bound.
Values may be sent and summed in bfloat16 or wider, within the bound.
A program may use at most 128 MiB of HBM per device.

v0:
```python
import jax
import jax.numpy as jnp
from jax import lax
from jax.sharding import PartitionSpec as P

HEAD_DIM = 64


norm_eps = 1e-06
block_images = 4


def normalize(values):
    center = values - jnp.mean(values, axis=-1, keepdims=True)
    inverse = lax.rsqrt(jnp.mean(center * center, axis=-1, keepdims=True) + norm_eps)
    return (center * inverse, inverse)


def norm_back(grad_norm, normed, inverse):
    mean_grad = jnp.mean(grad_norm, axis=-1, keepdims=True)
    mean_proj = jnp.mean(grad_norm * normed, axis=-1, keepdims=True)
    return inverse * (grad_norm - mean_grad - normed * mean_proj)


def gelu_exact(values):
    return jax.nn.gelu(values, approximate=False)


def attention_forward(block_in, weights):
    (
        attention_gain,
        attention_shift,
        input_weight,
        query_bias,
        value_bias,
        output_weight,
        output_bias,
        feed_gain,
        feed_shift,
        up_weight,
        up_bias,
        down_weight,
        down_bias,
    ) = weights
    images, seq_len, model_width = block_in.shape
    row_total = images * seq_len
    head_count = model_width // HEAD_DIM
    score_scale = HEAD_DIM ** (-0.5)
    stream_in = block_in.astype(jnp.float32).reshape(row_total, model_width)
    normed_a, inverse_a = normalize(stream_in)
    input_a = (normed_a * attention_gain + attention_shift).astype(jnp.bfloat16)
    bias_full = jnp.concatenate([query_bias, jnp.zeros_like(query_bias), value_bias])
    mixed_low = (
        jnp.dot(input_a, input_weight, preferred_element_type=jnp.float32) + bias_full
    ).astype(jnp.bfloat16)
    split_heads = mixed_low.reshape(images, seq_len, 3, head_count, HEAD_DIM)
    query_rows = split_heads[:, :, 0]
    key_rows = split_heads[:, :, 1]
    value_rows = split_heads[:, :, 2]
    scores = (
        jnp.einsum("bqhe,bkhe->bhqk", query_rows, key_rows, preferred_element_type=jnp.float32)
        * score_scale
    )
    exp_scores = jnp.exp(scores)
    softmax_out = exp_scores / jnp.sum(exp_scores, axis=-1, keepdims=True)
    softmax_low = softmax_out.astype(jnp.bfloat16)
    context = jnp.einsum(
        "bhqk,bkhe->bqhe", softmax_low, value_rows, preferred_element_type=jnp.float32
    )
    context = context.astype(jnp.bfloat16).reshape(row_total, model_width)
    middle = (
        stream_in
        + jnp.dot(context, output_weight, preferred_element_type=jnp.float32)
        + output_bias
    )
    return (
        normed_a,
        inverse_a,
        input_a,
        query_rows,
        key_rows,
        value_rows,
        softmax_out,
        softmax_low,
        context,
        middle,
    )


def feed_forward(middle, weights):
    (
        attention_gain,
        attention_shift,
        input_weight,
        query_bias,
        value_bias,
        output_weight,
        output_bias,
        feed_gain,
        feed_shift,
        up_weight,
        up_bias,
        down_weight,
        down_bias,
    ) = weights
    normed_b, inverse_b = normalize(middle)
    input_b = (normed_b * feed_gain + feed_shift).astype(jnp.bfloat16)
    hidden_pre = jnp.dot(input_b, up_weight, preferred_element_type=jnp.float32) + up_bias
    hidden_low = gelu_exact(hidden_pre).astype(jnp.bfloat16)
    result = (
        middle + jnp.dot(hidden_low, down_weight, preferred_element_type=jnp.float32) + down_bias
    )
    return (normed_b, inverse_b, input_b, hidden_pre, hidden_low, result)


def feed_backward(grad_out, feed_state, weights):
    (
        attention_gain,
        attention_shift,
        input_weight,
        query_bias,
        value_bias,
        output_weight,
        output_bias,
        feed_gain,
        feed_shift,
        up_weight,
        up_bias,
        down_weight,
        down_bias,
    ) = weights
    normed_b, inverse_b, input_b, hidden_pre, hidden_low, result = feed_state
    grad_low = grad_out.astype(jnp.bfloat16)
    down_weight_grad = jnp.einsum(
        "rf,rd->fd", hidden_low, grad_low, preferred_element_type=jnp.float32
    )
    down_bias_grad = jnp.sum(grad_out, axis=0)
    grad_hidden = jnp.einsum("rd,fd->rf", grad_low, down_weight, preferred_element_type=jnp.float32)
    unused_value, gelu_pull = jax.vjp(gelu_exact, hidden_pre)
    grad_pre = gelu_pull(grad_hidden)[0].astype(jnp.bfloat16)
    up_weight_grad = jnp.einsum("rd,rf->df", input_b, grad_pre, preferred_element_type=jnp.float32)
    up_bias_grad = jnp.sum(grad_pre, axis=0, dtype=jnp.float32)
    grad_second = jnp.einsum("rf,df->rd", grad_pre, up_weight, preferred_element_type=jnp.float32)
    feed_gain_grad = jnp.sum(grad_second * normed_b, axis=0)
    feed_shift_grad = jnp.sum(grad_second, axis=0)
    grad_middle = grad_out + norm_back(grad_second * feed_gain, normed_b, inverse_b)
    return (
        grad_middle,
        (
            feed_gain_grad,
            feed_shift_grad,
            up_weight_grad,
            up_bias_grad,
            down_weight_grad,
            down_bias_grad,
        ),
    )


def attention_backward(grad_middle, attention_state, weights, images, seq_len):
    (
        attention_gain,
        attention_shift,
        input_weight,
        query_bias,
        value_bias,
        output_weight,
        output_bias,
        feed_gain,
        feed_shift,
        up_weight,
        up_bias,
        down_weight,
        down_bias,
    ) = weights
    (
        normed_a,
        inverse_a,
        input_a,
        query_rows,
        key_rows,
        value_rows,
        softmax_out,
        softmax_low,
        context,
        middle,
    ) = attention_state
    model_width = grad_middle.shape[1]
    row_total = images * seq_len
    head_count = model_width // HEAD_DIM
    score_scale = HEAD_DIM ** (-0.5)
    grad_branch = grad_middle.astype(jnp.bfloat16)
    output_weight_grad = jnp.einsum(
        "rd,re->de", context, grad_branch, preferred_element_type=jnp.float32
    )
    output_bias_grad = jnp.sum(grad_branch, axis=0, dtype=jnp.float32)
    grad_context = jnp.einsum(
        "re,de->rd", grad_branch, output_weight, preferred_element_type=jnp.float32
    )
    grad_context = grad_context.astype(jnp.bfloat16).reshape(images, seq_len, head_count, HEAD_DIM)
    grad_softmax = jnp.einsum(
        "bqhe,bkhe->bhqk", grad_context, value_rows, preferred_element_type=jnp.float32
    )
    grad_value = jnp.einsum(
        "bhqk,bqhe->bkhe", softmax_low, grad_context, preferred_element_type=jnp.float32
    )
    row_terms = jnp.sum(grad_softmax * softmax_out, axis=-1, keepdims=True)
    grad_scores = (softmax_out * (grad_softmax - row_terms)).astype(jnp.bfloat16)
    grad_query = (
        jnp.einsum("bhqk,bkhe->bqhe", grad_scores, key_rows, preferred_element_type=jnp.float32)
        * score_scale
    )
    grad_key = (
        jnp.einsum("bhqk,bqhe->bkhe", grad_scores, query_rows, preferred_element_type=jnp.float32)
        * score_scale
    )
    grad_mixed = jnp.stack([grad_query, grad_key, grad_value], axis=2).astype(jnp.bfloat16)
    grad_mixed = grad_mixed.reshape(row_total, 3 * model_width)
    input_weight_grad = jnp.einsum(
        "rd,re->de", input_a, grad_mixed, preferred_element_type=jnp.float32
    )
    query_bias_grad = jnp.sum(grad_mixed[:, :model_width], axis=0, dtype=jnp.float32)
    value_bias_grad = jnp.sum(grad_mixed[:, 2 * model_width :], axis=0, dtype=jnp.float32)
    grad_first = jnp.einsum(
        "re,de->rd", grad_mixed, input_weight, preferred_element_type=jnp.float32
    )
    attention_gain_grad = jnp.sum(grad_first * normed_a, axis=0)
    attention_shift_grad = jnp.sum(grad_first, axis=0)
    grad_stream = grad_middle + norm_back(grad_first * attention_gain, normed_a, inverse_a)
    return (
        grad_stream,
        (
            attention_gain_grad,
            attention_shift_grad,
            input_weight_grad,
            query_bias_grad,
            value_bias_grad,
            output_weight_grad,
            output_bias_grad,
        ),
    )


def shards(
    tokens,
    cotangent,
    image_count,
    attention_gain,
    attention_shift,
    input_weight,
    query_bias,
    value_bias,
    output_weight,
    output_bias,
    feed_gain,
    feed_shift,
    up_weight,
    up_bias,
    down_weight,
    down_bias,
):
    weights = (
        lax.all_gather(attention_gain, "shard", axis=0, tiled=True),
        lax.all_gather(attention_shift, "shard", axis=0, tiled=True),
        lax.all_gather(input_weight, "shard", axis=0, tiled=True),
        lax.all_gather(query_bias, "shard", axis=0, tiled=True),
        lax.all_gather(value_bias, "shard", axis=0, tiled=True),
        lax.all_gather(output_weight, "shard", axis=0, tiled=True),
        lax.all_gather(output_bias, "shard", axis=0, tiled=True),
        lax.all_gather(feed_gain, "shard", axis=0, tiled=True),
        lax.all_gather(feed_shift, "shard", axis=0, tiled=True),
        lax.all_gather(up_weight, "shard", axis=0, tiled=True),
        lax.all_gather(up_bias, "shard", axis=0, tiled=True),
        lax.all_gather(down_weight, "shard", axis=0, tiled=True),
        lax.all_gather(down_bias, "shard", axis=0, tiled=True),
    )
    live_count = image_count[0]
    block_total = tokens.shape[0] // block_images
    seq_len = tokens.shape[1]
    model_width = tokens.shape[2]
    zero_grads = tuple((jnp.zeros(piece.shape, jnp.float32) for piece in weights))

    def slot_mask(block_start):
        return block_start + jnp.arange(block_images) < live_count

    def masked_cot(block_start, cot_block):
        keep = slot_mask(block_start)[:, None, None]
        return jnp.where(keep, cot_block.astype(jnp.float32), 0.0).reshape(-1, model_width)

    def forward_and_feed(values, cot_block, block_start):
        attention_state = attention_forward(values, weights)
        feed_state = feed_forward(attention_state[-1], weights)
        keep = slot_mask(block_start)[:, None, None]
        out_block = jnp.where(keep, feed_state[-1].reshape(values.shape), 0.0).astype(jnp.bfloat16)
        grad_middle, feed_grads = feed_backward(
            masked_cot(block_start, cot_block), feed_state, weights
        )
        return (attention_state, out_block, grad_middle, feed_grads)

    def whole_step(block_index, carry):
        grad_total, outputs, tokens_grad = carry
        block_start = block_index * block_images
        block_in = lax.dynamic_slice_in_dim(tokens, block_start, block_images, 0)
        block_cot = lax.dynamic_slice_in_dim(cotangent, block_start, block_images, 0)

        def run_block(pair):
            values, cot_block = pair
            attention_state, out_block, grad_middle, feed_grads = forward_and_feed(
                values, cot_block, block_start
            )
            grad_stream, attention_grads = attention_backward(
                grad_middle, attention_state, weights, block_images, seq_len
            )
            return (
                out_block,
                grad_stream.astype(jnp.bfloat16).reshape(values.shape),
                attention_grads + feed_grads,
            )

        def skip_block(pair):
            return (jnp.zeros_like(pair[0]), jnp.zeros_like(pair[0]), zero_grads)

        out_block, grad_block, grad_parts = lax.cond(
            block_start < live_count, run_block, skip_block, (block_in, block_cot)
        )
        grad_total = jax.tree.map(jnp.add, grad_total, grad_parts)
        outputs = lax.dynamic_update_slice_in_dim(outputs, out_block, block_start, 0)
        tokens_grad = lax.dynamic_update_slice_in_dim(tokens_grad, grad_block, block_start, 0)
        return (grad_total, outputs, tokens_grad)

    grad_total, output, tokens_grad = lax.fori_loop(
        0, block_total, whole_step, (zero_grads, jnp.zeros_like(tokens), jnp.zeros_like(tokens))
    )
    summed = (
        lax.psum_scatter(grad_total[0], "shard", scatter_dimension=0, tiled=True),
        lax.psum_scatter(grad_total[1], "shard", scatter_dimension=0, tiled=True),
        lax.psum_scatter(grad_total[2], "shard", scatter_dimension=0, tiled=True),
        lax.psum_scatter(grad_total[3], "shard", scatter_dimension=0, tiled=True),
        lax.psum_scatter(grad_total[4], "shard", scatter_dimension=0, tiled=True),
        lax.psum_scatter(grad_total[5], "shard", scatter_dimension=0, tiled=True),
        lax.psum_scatter(grad_total[6], "shard", scatter_dimension=0, tiled=True),
        lax.psum_scatter(grad_total[7], "shard", scatter_dimension=0, tiled=True),
        lax.psum_scatter(grad_total[8], "shard", scatter_dimension=0, tiled=True),
        lax.psum_scatter(grad_total[9], "shard", scatter_dimension=0, tiled=True),
        lax.psum_scatter(grad_total[10], "shard", scatter_dimension=0, tiled=True),
        lax.psum_scatter(grad_total[11], "shard", scatter_dimension=0, tiled=True),
        lax.psum_scatter(grad_total[12], "shard", scatter_dimension=0, tiled=True),
    )
    return (output, tokens_grad) + tuple(summed)


def solution(mesh):
    placed = (
        P("shard", None, None),
        P("shard", None, None),
        P("shard"),
        P("shard"),
        P("shard"),
        P("shard", None),
        P("shard"),
        P("shard"),
        P("shard", None),
        P("shard"),
        P("shard"),
        P("shard"),
        P("shard", None),
        P("shard"),
        P("shard", None),
        P("shard"),
    )
    return jax.shard_map(
        shards,
        mesh=mesh,
        in_specs=placed,
        out_specs=(
            P("shard", None, None),
            P("shard", None, None),
            P("shard"),
            P("shard"),
            P("shard", None),
            P("shard"),
            P("shard"),
            P("shard", None),
            P("shard"),
            P("shard"),
            P("shard"),
            P("shard", None),
            P("shard"),
            P("shard", None),
            P("shard"),
        ),
        check_vma=False,
    )
```

profile of v0, /device:TPU:0, one launch (start us, length us, event | category | flops | bytes accessed | tf_op | source)
XLA Modules:
  0.0 735.3 jit_solution(3403910905440626225)
XLA Ops:
  9.0 47.1 %all-gather = bf16[32,12,1152]{2,1,0:T(8,128)(2,1)S(1)} all-gather(bf16[1,12,1152]{2,1,0:T(8,128)(2,1)} %bitcast.67), channel_id=1, replica_groups=mesh['shard'=32] {'shard'}, dimensions={0}, use_global_device_ids=true | all-gather | bytes 912384 | tf_op jit(solution)/shard_map/all_gather | solution.py:265
  57.2 37.9 %all-gather.1 = bf16[32,12,384]{2,1,0:T(8,128)(2,1)S(1)} all-gather(bf16[1,12,384]{2,1,0:T(8,128)(2,1)S(1)} %bitcast.68), channel_id=1, replica_groups=mesh['shard'=32] {'shard'}, dimensions={0}, use_global_device_ids=true | all-gather | bytes 304128 | tf_op jit(solution)/shard_map/all_gather | solution.py:268
  97.5 37.2 %all-reduce.25 = (bf16[384]{0:T(512)(128)(2,1)S(1)}, bf16[384]{0:T(512)(128)(2,1)S(1)}, bf16[384]{0:T(512)(128)(2,1)S(1)}, bf16[384]{0:T(512)(128)(2,1)S(1)}, bf...) all-reduce(bf16[384]{0:T(512)(128)(2,1)S(1)} %dynamic-update-slice,, ...), channel_id=1, replica_groups=mesh['shard'=32] {'shard'}, use_global_device_ids=true, to_apply=%add | all-reduce | flops 4608 | bytes 18432
  134.7 3.0 reshape.230
  140.5 384.8 %while.42 = (s32[]{:T(128)}, f32[384]{0:T(512)}, f32[384]{0:T(512)}, f32[384,1152]{1,0:T(8,128)}, f32[384]{0:T(512)}, /*index=5*/f32[384]{0:T(512)}, f32[384,384...) while((s32[]{:T(128)}, f32[384]{0:T(512)}, ...), condition=%wide.region_22.23_spmd.clone, body=%wide.region_0.22_spmd.clone.sunk | while | flops 9233007616 | bytes 313996832 | solution.py:331
  141.2 110.4 %conditional.3 = (bf16[4,197,384]{2,1,0:T(8,128)(2,1)}, bf16[4,197,384]{2,1,0:T(8,128)(2,1)}, f32[384]{0:T(512)S(1)}, f32[384]{0:T(512)S(1)}, f32[384,1152]{1,0:...) conditional(s32[]{:T(128)} %convert_element_type.224, () %tuple.88, ...), branch_computations={%region_1.0_spmd, %region_2.21_spmd} | conditional | flops 9229457408 | bytes 252352032 | solution.py:323
  148.4 4.8 reshape.231
  153.2 5.0 fusion.42
  162.5 3.3 fusion.10
  168.6 3.5 fusion.14
  175.3 14.3 %multiply_convert_fusion.1 = (bf16[788,1536]{1,0:T(8,128)(2,1)}, f32[788,1536]{1,0:T(8,128)}, f32[788,1536]{1,0:T(8,128)}) fusion(f32[1536]{0:T(1024)S(1)} %convert_element_type.156, bf16[384,1536]{1,0:T(8,128)(2,1)S(1)} %copy-done.19, f32[788,384]{1,0:T(8,128)S(1)} %get-tuple-element.917, f32[384]{0:T(512)S(1)} %convert_element_type.154, ...), kind=kOutput, calls=%fused_computation.7 | convolution fusion | flops 1010959872 | bytes 14509216 | tf_op jit(solution)/shard_map/while/body/eval_jaxpr/cond/branch_1_fun/dot_general | solution.py:108
  190.3 3.1 fusion.35
  194.5 7.4 %convert_reduce_fusion = (f32[1536]{0:T(1024)S(1)}, bf16[788,1536]{1,0:T(8,128)(2,1)S(1)}) fusion(f32[788,1536]{1,0:T(8,128)} %get-tuple-element.908, bf16[1536,384]{1,0:T(8,128)(2,1)} %get-tuple-element.597, f32[788,384]{1,0:T(8,128)} %reshape.204, f32[788,1536]{1,0:T(8,128)} %get-tuple-element.918, f32[1536]{0:T(1024)S(1)} %convert_element_type.156), kind=kOutput, calls=%fused_computation.5 | convolution fusion | flops 950439936 | bytes 14505984 | tf_op jit(solution)/shard_map/while/body/eval_jaxpr/cond/branch_1_fun/rd,fd->rf/dot_general | solution.py:138
  202.0 3.0 fusion.36
  214.6 4.4 multiply_reduce_fusion
  224.0 3.4 copy.65
  227.5 5.6 convert_element_type.167
  234.1 4.4 fusion.44
  243.6 5.0 fusion.29
  254.3 3.6 select_add_fusion.28
  267.7 110.3 %conditional.3 = (bf16[4,197,384]{2,1,0:T(8,128)(2,1)}, bf16[4,197,384]{2,1,0:T(8,128)(2,1)}, f32[384]{0:T(512)S(1)}, f32[384]{0:T(512)S(1)}, f32[384,1152]{1,0:...) conditional(s32[]{:T(128)} %convert_element_type.224, () %tuple.88, ...), branch_computations={%region_1.0_spmd, %region_2.21_spmd} | conditional | flops 9229457408 | bytes 252352032 | solution.py:323
  274.9 4.8 reshape.231
  279.7 5.0 fusion.42
  289.3 3.3 fusion.10
  295.4 3.5 fusion.14
  302.0 13.9 %multiply_convert_fusion.1 = (bf16[788,1536]{1,0:T(8,128)(2,1)}, f32[788,1536]{1,0:T(8,128)}, f32[788,1536]{1,0:T(8,128)}) fusion(f32[1536]{0:T(1024)S(1)} %convert_element_type.156, bf16[384,1536]{1,0:T(8,128)(2,1)S(1)} %copy-done.19, f32[788,384]{1,0:T(8,128)S(1)} %get-tuple-element.917, f32[384]{0:T(512)S(1)} %convert_element_type.154, ...), kind=kOutput, calls=%fused_computation.7 | convolution fusion | flops 1010959872 | bytes 14509216 | tf_op jit(solution)/shard_map/while/body/eval_jaxpr/cond/branch_1_fun/dot_general | solution.py:108
  316.6 3.1 fusion.35
  320.9 7.4 %convert_reduce_fusion = (f32[1536]{0:T(1024)S(1)}, bf16[788,1536]{1,0:T(8,128)(2,1)S(1)}) fusion(f32[788,1536]{1,0:T(8,128)} %get-tuple-element.908, bf16[1536,384]{1,0:T(8,128)(2,1)} %get-tuple-element.597, f32[788,384]{1,0:T(8,128)} %reshape.204, f32[788,1536]{1,0:T(8,128)} %get-tuple-element.918, f32[1536]{0:T(1024)S(1)} %convert_element_type.156), kind=kOutput, calls=%fused_computation.5 | convolution fusion | flops 950439936 | bytes 14505984 | tf_op jit(solution)/shard_map/while/body/eval_jaxpr/cond/branch_1_fun/rd,fd->rf/dot_general | solution.py:138
  328.3 3.0 fusion.36
  338.0 2.9 copy.60
  341.0 4.4 multiply_reduce_fusion
  350.4 3.4 copy.65
  353.8 5.7 convert_element_type.167
  360.5 4.4 fusion.44
  370.0 5.0 fusion.29
  380.8 4.3 select_add_fusion.28
  395.1 110.3 %conditional.3 = (bf16[4,197,384]{2,1,0:T(8,128)(2,1)}, bf16[4,197,384]{2,1,0:T(8,128)(2,1)}, f32[384]{0:T(512)S(1)}, f32[384]{0:T(512)S(1)}, f32[384,1152]{1,0:...) conditional(s32[]{:T(128)} %convert_element_type.224, () %tuple.88, ...), branch_computations={%region_1.0_spmd, %region_2.21_spmd} | conditional | flops 9229457408 | bytes 252352032 | solution.py:323
  402.3 4.8 reshape.231
  407.1 5.0 fusion.42
  416.3 3.3 fusion.10
  422.4 3.5 fusion.14
  429.0 13.9 %multiply_convert_fusion.1 = (bf16[788,1536]{1,0:T(8,128)(2,1)}, f32[788,1536]{1,0:T(8,128)}, f32[788,1536]{1,0:T(8,128)}) fusion(f32[1536]{0:T(1024)S(1)} %convert_element_type.156, bf16[384,1536]{1,0:T(8,128)(2,1)S(1)} %copy-done.19, f32[788,384]{1,0:T(8,128)S(1)} %get-tuple-element.917, f32[384]{0:T(512)S(1)} %convert_element_type.154, ...), kind=kOutput, calls=%fused_computation.7 | convolution fusion | flops 1010959872 | bytes 14509216 | tf_op jit(solution)/shard_map/while/body/eval_jaxpr/cond/branch_1_fun/dot_general | solution.py:108
  443.7 3.1 fusion.35
  447.9 7.4 %convert_reduce_fusion = (f32[1536]{0:T(1024)S(1)}, bf16[788,1536]{1,0:T(8,128)(2,1)S(1)}) fusion(f32[788,1536]{1,0:T(8,128)} %get-tuple-element.908, bf16[1536,384]{1,0:T(8,128)(2,1)} %get-tuple-element.597, f32[788,384]{1,0:T(8,128)} %reshape.204, f32[788,1536]{1,0:T(8,128)} %get-tuple-element.918, f32[1536]{0:T(1024)S(1)} %convert_element_type.156), kind=kOutput, calls=%fused_computation.5 | convolution fusion | flops 950439936 | bytes 14505984 | tf_op jit(solution)/shard_map/while/body/eval_jaxpr/cond/branch_1_fun/rd,fd->rf/dot_general | solution.py:138
  455.3 3.0 fusion.36
  465.1 3.0 copy.60
  468.1 4.4 multiply_reduce_fusion
  477.5 3.4 copy.65
  480.9 5.7 convert_element_type.167
  487.7 4.4 fusion.44
  497.1 5.0 fusion.29
  508.2 4.3 select_add_fusion.28
  527.1 84.3 %fusion.40 = (f32[16,1152]{1,0:T(8,128)S(1)}, f32[16,384]{1,0:T(8,128)S(1)}, f32[16,1536]{1,0:T(8,128)S(1)}) fusion(f32[384,1152]{1,0:T(8,128)} %get-tuple-element.682, f32[384,384]{1,0:T(8,128)} %get-tuple-element.685, f32[384,1536]{1,0:T(8,128)S(1)} %copy-done.11), kind=kCustom, calls=%all-reduce-scatter.3 | all-reduce-scatter fusion | flops 1572865 | bytes 4915200
  621.1 4.9 collective-permute-start.13
  626.1 3.6 collective-permute-start.14
  635.1 3.0 collective-permute-start
  638.2 3.7 collective-permute-start.1
  644.0 3.2 collective-permute-start.3
  648.6 37.6 %all-reduce.24 = (f32[384]{0:T(512)S(1)}, f32[384]{0:T(512)S(1)}, f32[384]{0:T(512)S(1)}, f32[384]{0:T(512)S(1)}, f32[384]{0:T(512)S(1)}, /*index=5*/f32[384]{0:...) all-reduce(f32[384]{0:T(512)S(1)} %copy-done.28, ...), channel_id=2, replica_groups=mesh['shard'=32] {'shard'}, use_global_device_ids=true, to_apply=%region_23.24.clone | all-reduce | flops 4608 | bytes 36864
  693.7 4.8 collective-permute-start.17
  698.5 4.5 collective-permute-start.5
  703.0 3.6 collective-permute-start.6
  711.8 3.1 collective-permute-start.19
  718.8 3.8 collective-permute-start.21
  (670 shorter events, 205.5 us)
Async XLA Ops:
  7.2 50.1 %copy-start.63 = (bf16[12,384]{1,0:T(8,128)(2,1)S(1)}, bf16[12,384]{1,0:T(8,128)(2,1)}, u32[]{:S(2)}) copy-start(bf16[12,384]{1,0:T(8,128)(2,1)} %param.28) | copy-start | bytes 27652
  7.2 88.0 %copy-start.65 = (bf16[12]{0:T(256)(128)(2,1)S(1)}, bf16[12]{0:T(256)(128)(2,1)}, u32[]{:S(2)}) copy-start(bf16[12]{0:T(256)(128)(2,1)} %param.23) | copy-start | bytes 76
  7.2 88.3 %copy-start.66 = (bf16[12]{0:T(256)(128)(2,1)S(1)}, bf16[12]{0:T(256)(128)(2,1)}, u32[]{:S(2)}) copy-start(bf16[12]{0:T(256)(128)(2,1)} %param.24) | copy-start | bytes 76
  7.2 88.5 %copy-start.67 = (bf16[12]{0:T(256)(128)(2,1)S(1)}, bf16[12]{0:T(256)(128)(2,1)}, u32[]{:S(2)}) copy-start(bf16[12]{0:T(256)(128)(2,1)} %param.26) | copy-start | bytes 76
  7.2 88.7 %copy-start.68 = (bf16[12]{0:T(256)(128)(2,1)S(1)}, bf16[12]{0:T(256)(128)(2,1)}, u32[]{:S(2)}) copy-start(bf16[12]{0:T(256)(128)(2,1)} %param.27) | copy-start | bytes 76
  7.2 89.0 %copy-start.69 = (bf16[12]{0:T(256)(128)(2,1)S(1)}, bf16[12]{0:T(256)(128)(2,1)}, u32[]{:S(2)}) copy-start(bf16[12]{0:T(256)(128)(2,1)} %param.29) | copy-start | bytes 76
  7.2 89.2 %copy-start.70 = (bf16[12]{0:T(256)(128)(2,1)S(1)}, bf16[12]{0:T(256)(128)(2,1)}, u32[]{:S(2)}) copy-start(bf16[12]{0:T(256)(128)(2,1)} %param.30) | copy-start | bytes 76
  7.3 89.5 %copy-start.71 = (bf16[12]{0:T(256)(128)(2,1)S(1)}, bf16[12]{0:T(256)(128)(2,1)}, u32[]{:S(2)}) copy-start(bf16[12]{0:T(256)(128)(2,1)} %param.31) | copy-start | bytes 76
  7.3 89.7 %copy-start.72 = (bf16[12]{0:T(256)(128)(2,1)S(1)}, bf16[12]{0:T(256)(128)(2,1)}, u32[]{:S(2)}) copy-start(bf16[12]{0:T(256)(128)(2,1)} %param.35) | copy-start | bytes 76
  7.3 89.9 %copy-start.73 = (bf16[48]{0:T(256)(128)(2,1)S(1)}, bf16[48]{0:T(256)(128)(2,1)}, u32[]{:S(2)}) copy-start(bf16[48]{0:T(256)(128)(2,1)} %param.33) | copy-start | bytes 292
  7.3 127.4 %all-gather.8.cloned.1.call-start = ((), (), s32[]{:S(2)}) async-start(), calls=%async_computation.3 | async-start | bytes 1622016 | tf_op jit(solution)/shard_map/all_gather | solution.py:272
  8.0 129.7 %all-gather.6.cloned.1.call-start = ((), (), s32[]{:S(2)}) async-start(), calls=%async_computation.1 | async-start | bytes 1216512 | tf_op jit(solution)/shard_map/all_gather | solution.py:274
  8.8 719.8 %reduce-scatter.8.cloned.1.call-start = ((), (), s32[]{:S(2)}) async-start(), calls=%async_computation.2 | async-start | bytes 2433024 | tf_op jit(solution)/shard_map/reduce_scatter | solution.py:346
  145.5 28.6 %copy-start = (f32[788,384]{1,0:T(8,128)}, f32[788,384]{1,0:T(8,128)S(1)}, u32[]{:S(2)}) copy-start(f32[788,384]{1,0:T(8,128)S(1)} %reshape.200) | copy-start | bytes 3631108 | tf_op jit(solution)/shard_map/while/body/eval_jaxpr/cond
  211.7 7.3 slice-start
  260.5 6.2 copy-start.25
  260.5 6.2 copy-start.53
  260.5 6.1 copy-start.55
  260.5 6.1 copy-start.60
  260.5 6.1 copy-start.62
  272.0 28.8 %copy-start = (f32[788,384]{1,0:T(8,128)}, f32[788,384]{1,0:T(8,128)S(1)}, u32[]{:S(2)}) copy-start(f32[788,384]{1,0:T(8,128)S(1)} %reshape.200) | copy-start | bytes 3631108 | tf_op jit(solution)/shard_map/while/body/eval_jaxpr/cond
  338.0 7.4 slice-start
  387.6 6.2 copy-start.25
  387.7 6.2 copy-start.53
  387.7 6.1 copy-start.55
  387.7 6.1 copy-start.60
  399.4 28.5 %copy-start = (f32[788,384]{1,0:T(8,128)}, f32[788,384]{1,0:T(8,128)S(1)}, u32[]{:S(2)}) copy-start(f32[788,384]{1,0:T(8,128)S(1)} %reshape.200) | copy-start | bytes 3631108 | tf_op jit(solution)/shard_map/while/body/eval_jaxpr/cond
  465.1 7.4 %slice-start = ((s8[4915200]{0:T(1024)(128)(4,1)}), s8[720896]{0:T(1024)(128)(4,1)S(1)}, s32[]{:S(2)}) async-start(s8[4915200]{0:T(1024)(128)(4,1)} %bitcast.64), calls=%async_computation.4 | async-start | bytes 1441792 | tf_op jit(solution)/shard_map/while/body/eval_jaxpr/cond
  515.0 6.2 copy-start.25
  515.0 6.2 copy-start.53
  515.1 6.1 copy-start.55
  515.1 6.1 copy-start.60
  527.0 121.5 %copy-start.28 = (f32[384]{0:T(512)S(1)}, f32[384]{0:T(512)}, u32[]{:S(2)}) copy-start(f32[384]{0:T(512)} %get-tuple-element.680) | copy-start | bytes 4612
  527.0 121.5 %copy-start.31 = (f32[384]{0:T(512)S(1)}, f32[384]{0:T(512)}, u32[]{:S(2)}) copy-start(f32[384]{0:T(512)} %get-tuple-element.681) | copy-start | bytes 4612
  527.0 121.5 %copy-start.34 = (f32[384]{0:T(512)S(1)}, f32[384]{0:T(512)}, u32[]{:S(2)}) copy-start(f32[384]{0:T(512)} %get-tuple-element.692) | copy-start | bytes 4612
  527.0 121.5 %copy-start.37 = (f32[384]{0:T(512)S(1)}, f32[384]{0:T(512)}, u32[]{:S(2)}) copy-start(f32[384]{0:T(512)} %get-tuple-element.683) | copy-start | bytes 4612
  527.0 121.5 %copy-start.40 = (f32[384]{0:T(512)S(1)}, f32[384]{0:T(512)}, u32[]{:S(2)}) copy-start(f32[384]{0:T(512)} %get-tuple-element.684) | copy-start | bytes 4612
  527.0 121.5 %copy-start.43 = (f32[384]{0:T(512)S(1)}, f32[384]{0:T(512)}, u32[]{:S(2)}) copy-start(f32[384]{0:T(512)} %get-tuple-element.686) | copy-start | bytes 4612
  527.0 121.5 %copy-start.46 = (f32[384]{0:T(512)S(1)}, f32[384]{0:T(512)}, u32[]{:S(2)}) copy-start(f32[384]{0:T(512)} %get-tuple-element.687) | copy-start | bytes 4612
  527.0 121.5 %copy-start.49 = (f32[384]{0:T(512)S(1)}, f32[384]{0:T(512)}, u32[]{:S(2)}) copy-start(f32[384]{0:T(512)} %get-tuple-element.688) | copy-start | bytes 4612
  611.3 35.8 %collective-permute-start.7 = (f32[12,1152]{1,0:T(8,128)S(1)}, f32[12,1152]{1,0:T(8,128)S(1)}, u32[]{:S(2)}, u32[]{:S(2)}) collective-permute-start(f32[12,1152]{1,0:T(8,128)S(1)} %slice.30), channel_id=1, source_target_pairs={{0,8},{1,9},{2,10},{3,11},{4,12},{5,13},{6,14},{7,15},{8,16},{9,17... | collective-permute-start | bytes 165896
  612.6 13.4 %collective-permute-start.10 = (f32[16,384]{1,0:T(8,128)S(1)}, f32[16,384]{1,0:T(8,128)S(1)}, u32[]{:S(2)}, u32[]{:S(2)}) collective-permute-start(f32[16,384]{1,0:T(8,128)S(1)} %get-tuple-element.903), channel_id=1, source_target_pairs={{0,3},{1,4},{2,5},{3,6},{4,7},{5,8},{6,9},{7,10},{8,11},{9,12},{10... | collective-permute-start | bytes 73736
  613.9 15.8 %collective-permute-start.11 = (f32[16,384]{1,0:T(8,128)S(1)}, f32[16,384]{1,0:T(8,128)S(1)}, u32[]{:S(2)}, u32[]{:S(2)}) collective-permute-start(f32[16,384]{1,0:T(8,128)S(1)} %get-tuple-element.903), channel_id=1, source_target_pairs={{0,4},{1,5},{2,6},{3,7},{4,8},{5,9},{6,10},{7,11},{8,12},{9,13},{1... | collective-permute-start | bytes 73736
  615.2 17.3 %collective-permute-start.12 = (f32[16,384]{1,0:T(8,128)S(1)}, f32[16,384]{1,0:T(8,128)S(1)}, u32[]{:S(2)}, u32[]{:S(2)}) collective-permute-start(f32[16,384]{1,0:T(8,128)S(1)} %get-tuple-element.903), channel_id=1, source_target_pairs={{0,5},{1,6},{2,7},{3,8},{4,9},{5,10},{6,11},{7,12},{8,13},{9,14},{... | collective-permute-start | bytes 73736
  617.0 4.1 collective-permute-start.15
  621.1 14.0 %collective-permute-start.13 = (f32[16,384]{1,0:T(8,128)S(1)}, f32[16,384]{1,0:T(8,128)S(1)}, u32[]{:S(2)}, u32[]{:S(2)}) collective-permute-start(f32[16,384]{1,0:T(8,128)S(1)} %get-tuple-element.903), channel_id=1, source_target_pairs={{0,6},{1,7},{2,8},{3,9},{4,10},{5,11},{6,12},{7,13},{8,14},{9,15},... | collective-permute-start | bytes 73736
  626.1 12.1 %collective-permute-start.14 = (f32[16,384]{1,0:T(8,128)S(1)}, f32[16,384]{1,0:T(8,128)S(1)}, u32[]{:S(2)}, u32[]{:S(2)}) collective-permute-start(f32[16,384]{1,0:T(8,128)S(1)} %get-tuple-element.903), channel_id=1, source_target_pairs={{0,7},{1,8},{2,9},{3,10},{4,11},{5,12},{6,13},{7,14},{8,15},{9,16}... | collective-permute-start | bytes 73736
  629.7 12.1 %collective-permute-start.8 = (f32[16,384]{1,0:T(8,128)S(1)}, f32[16,384]{1,0:T(8,128)S(1)}, u32[]{:S(2)}, u32[]{:S(2)}) collective-permute-start(f32[16,384]{1,0:T(8,128)S(1)} %get-tuple-element.903), channel_id=1, source_target_pairs={{0,1},{1,2},{2,3},{3,4},{4,5},{5,6},{6,7},{7,8},{8,9},{9,10},{10,1... | collective-permute-start | bytes 73736
  632.5 11.4 %collective-permute-start.9 = (f32[16,384]{1,0:T(8,128)S(1)}, f32[16,384]{1,0:T(8,128)S(1)}, u32[]{:S(2)}, u32[]{:S(2)}) collective-permute-start(f32[16,384]{1,0:T(8,128)S(1)} %get-tuple-element.903), channel_id=1, source_target_pairs={{0,2},{1,3},{2,4},{3,5},{4,6},{5,7},{6,8},{7,9},{8,10},{9,11},{10,... | collective-permute-start | bytes 73736
  635.1 57.2 %collective-permute-start = (f32[16,1152]{1,0:T(8,128)S(1)}, f32[16,1152]{1,0:T(8,128)S(1)}, u32[]{:S(2)}, u32[]{:S(2)}) collective-permute-start(f32[16,1152]{1,0:T(8,128)S(1)} %get-tuple-element.902), channel_id=1, source_target_pairs={{0,1},{1,2},{2,3},{3,4},{4,5},{5,6},{6,7},{7,8},{8,9},{9,10},{10,1... | collective-permute-start | bytes 221192
  638.2 55.5 %collective-permute-start.1 = (f32[16,1152]{1,0:T(8,128)S(1)}, f32[16,1152]{1,0:T(8,128)S(1)}, u32[]{:S(2)}, u32[]{:S(2)}) collective-permute-start(f32[16,1152]{1,0:T(8,128)S(1)} %get-tuple-element.902), channel_id=1, source_target_pairs={{0,2},{1,3},{2,4},{3,5},{4,6},{5,7},{6,8},{7,9},{8,10},{9,11},{10,... | collective-permute-start | bytes 221192
  641.8 56.7 %collective-permute-start.2 = (f32[16,1152]{1,0:T(8,128)S(1)}, f32[16,1152]{1,0:T(8,128)S(1)}, u32[]{:S(2)}, u32[]{:S(2)}) collective-permute-start(f32[16,1152]{1,0:T(8,128)S(1)} %get-tuple-element.902), channel_id=1, source_target_pairs={{0,3},{1,4},{2,5},{3,6},{4,7},{5,8},{6,9},{7,10},{8,11},{9,12},{10... | collective-permute-start | bytes 221192
  644.0 59.0 %collective-permute-start.3 = (f32[16,1152]{1,0:T(8,128)S(1)}, f32[16,1152]{1,0:T(8,128)S(1)}, u32[]{:S(2)}, u32[]{:S(2)}) collective-permute-start(f32[16,1152]{1,0:T(8,128)S(1)} %get-tuple-element.902), channel_id=1, source_target_pairs={{0,4},{1,5},{2,6},{3,7},{4,8},{5,9},{6,10},{7,11},{8,12},{9,13},{1... | collective-permute-start | bytes 221192
  647.2 59.5 %collective-permute-start.4 = (f32[16,1152]{1,0:T(8,128)S(1)}, f32[16,1152]{1,0:T(8,128)S(1)}, u32[]{:S(2)}, u32[]{:S(2)}) collective-permute-start(f32[16,1152]{1,0:T(8,128)S(1)} %get-tuple-element.902), channel_id=1, source_target_pairs={{0,5},{1,6},{2,7},{3,8},{4,9},{5,10},{6,11},{7,12},{8,13},{9,14},{... | collective-permute-start | bytes 221192
  692.4 26.4 %collective-permute-start.16 = (f32[16,1536]{1,0:T(8,128)S(1)}, f32[16,1536]{1,0:T(8,128)S(1)}, u32[]{:S(2)}, u32[]{:S(2)}) collective-permute-start(f32[16,1536]{1,0:T(8,128)S(1)} %get-tuple-element.904), channel_id=1, source_target_pairs={{0,1},{1,2},{2,3},{3,4},{4,5},{5,6},{6,7},{7,8},{8,9},{9,10},{10,1... | collective-permute-start | bytes 294920
  693.7 28.9 %collective-permute-start.17 = (f32[16,1536]{1,0:T(8,128)S(1)}, f32[16,1536]{1,0:T(8,128)S(1)}, u32[]{:S(2)}, u32[]{:S(2)}) collective-permute-start(f32[16,1536]{1,0:T(8,128)S(1)} %get-tuple-element.904), channel_id=1, source_target_pairs={{0,2},{1,3},{2,4},{3,5},{4,6},{5,7},{6,8},{7,9},{8,10},{9,11},{10,... | collective-permute-start | bytes 294920
  698.5 11.3 %collective-permute-start.5 = (f32[16,1152]{1,0:T(8,128)S(1)}, f32[16,1152]{1,0:T(8,128)S(1)}, u32[]{:S(2)}, u32[]{:S(2)}) collective-permute-start(f32[16,1152]{1,0:T(8,128)S(1)} %get-tuple-element.902), channel_id=1, source_target_pairs={{0,6},{1,7},{2,8},{3,9},{4,10},{5,11},{6,12},{7,13},{8,14},{9,15},... | collective-permute-start | bytes 221192
  703.0 8.8 %collective-permute-start.6 = (f32[16,1152]{1,0:T(8,128)S(1)}, f32[16,1152]{1,0:T(8,128)S(1)}, u32[]{:S(2)}, u32[]{:S(2)}) collective-permute-start(f32[16,1152]{1,0:T(8,128)S(1)} %get-tuple-element.902), channel_id=1, source_target_pairs={{0,7},{1,8},{2,9},{3,10},{4,11},{5,12},{6,13},{7,14},{8,15},{9,16}... | collective-permute-start | bytes 221192
  706.6 9.4 %collective-permute-start.23 = (f32[12,1536]{1,0:T(8,128)S(1)}, f32[12,1536]{1,0:T(8,128)S(1)}, u32[]{:S(2)}, u32[]{:S(2)}) collective-permute-start(f32[12,1536]{1,0:T(8,128)S(1)} %slice.32), channel_id=1, source_target_pairs={{0,8},{1,9},{2,10},{3,11},{4,12},{5,13},{6,14},{7,15},{8,16},{9,17... | collective-permute-start | bytes 221192
  709.8 15.3 %collective-permute-start.18 = (f32[16,1536]{1,0:T(8,128)S(1)}, f32[16,1536]{1,0:T(8,128)S(1)}, u32[]{:S(2)}, u32[]{:S(2)}) collective-permute-start(f32[16,1536]{1,0:T(8,128)S(1)} %get-tuple-element.904), channel_id=1, source_target_pairs={{0,3},{1,4},{2,5},{3,6},{4,7},{5,8},{6,9},{7,10},{8,11},{9,12},{10... | collective-permute-start | bytes 294920
  711.8 13.4 %collective-permute-start.19 = (f32[16,1536]{1,0:T(8,128)S(1)}, f32[16,1536]{1,0:T(8,128)S(1)}, u32[]{:S(2)}, u32[]{:S(2)}) collective-permute-start(f32[16,1536]{1,0:T(8,128)S(1)} %get-tuple-element.904), channel_id=1, source_target_pairs={{0,4},{1,5},{2,6},{3,7},{4,8},{5,9},{6,10},{7,11},{8,12},{9,13},{1... | collective-permute-start | bytes 294920
  716.0 9.2 %collective-permute-start.20 = (f32[16,1536]{1,0:T(8,128)S(1)}, f32[16,1536]{1,0:T(8,128)S(1)}, u32[]{:S(2)}, u32[]{:S(2)}) collective-permute-start(f32[16,1536]{1,0:T(8,128)S(1)} %get-tuple-element.904), channel_id=1, source_target_pairs={{0,5},{1,6},{2,7},{3,8},{4,9},{5,10},{6,11},{7,12},{8,13},{9,14},{... | collective-permute-start | bytes 294920
  718.8 6.4 collective-permute-start.21
  722.6 4.1 collective-permute-start.22
  (156 other events, 456.1 us)
Sparse Core Ops, SparseCore 0:
  11.0 59.2 all-gather.7
  73.1 52.9 all-gather.5
  525.5 108.2 reduce-scatter.7
where the time goes:
time: 743 us; the launch traced here: 735 us
  blocking collectives  244 us (33%)
  matrix products  176 us (24%)
  local copies, waits for them, and re-layouts  145 us (20%)
  other arithmetic  74.5 us (10%)
  starting transfers between devices  65.5 us (9%)
  between operations  14.7 us (2%)
  loops' own time  10.8 us (1%)
    unnamed x3, blocking collectives  159 us
    unnamed x24, starting transfers between devices  65.4 us
    all_gather x1, blocking collectives, shards(): lax.all_gather(input_weight, 'shard', axis=0, tiled=True)  47.1 us
    dot_general x3, matrix products, feed_forward(): jnp.dot(input_b, up_weight, preferred_element_type=jnp.float32) + up_bias  42.2 us
    all_gather x1, blocking collectives, shards(): lax.all_gather(output_weight, 'shard', axis=0, tiled=True)  37.9 us
    add x27, other arithmetic, whole_step(): grad_total = jax.tree.map(jnp.add, grad_total, grad_parts)  31.8 us
    convert_element_type x6, local copies, waits for them, and re-layouts, attention_backward(): jnp.stack([grad_query, grad_key, grad_value], axis=2).astype(jnp.bfloat16)  27.3 us
    cond x165, local copies, waits for them, and re-layouts  24.2 us
  transfers between devices with their start and end apart: 27, of which 2 were waited for; matrix products, arithmetic and copies ran while one was open for 14% of the time, Pallas kernels for 0%

commit v1 on v0

v1 whole, which is shorter than its diff:
```python
import functools
import math

import jax
import jax.numpy as jnp
from jax import lax
from jax.experimental import pallas as pl
from jax.experimental.pallas import tpu as pltpu
from jax.sharding import PartitionSpec as P

f32, bf16 = jnp.float32, jnp.bfloat16
HEAD_DIM = 64
EPS = 1e-06
LOG2E = math.log2(math.e)
SCALE = HEAD_DIM**-0.5
Z = 4
LANES = 128
AG, AS, QB, VB, OB, FG, FS, DB = range(8)


def nn(a, b):
    return jnp.dot(a, b, preferred_element_type=f32)


def nt(a, b):
    return lax.dot_general(a, b, (((1,), (1,)), ((), ())), preferred_element_type=f32)


def tn(a, b):
    return lax.dot_general(a, b, (((0,), (0,)), ((), ())), preferred_element_type=f32)


def normalize(x):
    c = x - jnp.mean(x, axis=-1, keepdims=True)
    inv = lax.rsqrt(jnp.mean(c * c, axis=-1, keepdims=True) + EPS)
    return c * inv, inv


def norm_back(w, n, inv):
    return inv * (w - jnp.mean(w, axis=-1, keepdims=True) - n * jnp.mean(w * n, axis=-1, keepdims=True))


def fold8(v):
    rows, cols = v.shape
    return jnp.sum(v.reshape(rows // 8, 8, cols), axis=0)


def pad_rows(v, rows):
    return jnp.concatenate([v, jnp.zeros((rows - v.shape[0], v.shape[1]), v.dtype)], axis=0)


class Place:
    def __init__(self, n):
        self.n, self.s = n, math.isqrt(n // (2 * Z))
        s = self.s
        me = lax.axis_index("shard")
        self.c = lax.rem(me, 2)
        q = lax.rem(lax.div(me, 2), s)
        p = lax.rem(lax.div(me, 2 * s), s)
        self.a = lax.div(me, 2 * s * s)
        self.f = p * (1 - self.c) + q * self.c
        self.g = q * (1 - self.c) + p * self.c

    def pq(self, f, g):
        return f * (1 - self.c) + g * self.c, g * (1 - self.c) + f * self.c

    def dev(self, a, f, g, c):
        p, q = self.pq(f, g)
        return ((a * self.s + p) * self.s + q) * 2 + c

    def around_a(self, k):
        return lax.rem(self.a + k, Z)

    def around_f(self, k):
        return lax.rem(self.f + k, self.s)

    def around_g(self, k):
        return lax.rem(self.g + k, self.s)

    def peers(self):
        s = self.s
        out = [self.dev(self.around_a(k), self.f, self.g, self.c) for k in range(1, Z)]
        out += [self.dev(self.a, self.around_f(k), self.g, self.c) for k in range(1, s)]
        out += [self.dev(self.a, self.f, self.around_g(k), self.c) for k in range(1, s)]
        p, q = self.pq(self.f, self.g)
        out.append(((self.a * s + p) * s + q) * 2 + 1 - self.c)
        return out


class Sems:
    def __init__(self, send, recv, local):
        self.send, self.recv, self.local, self.used, self.used_local = send, recv, local, 0, 0

    def take(self):
        self.used += 1
        return self.used - 1

    def take_local(self):
        self.used_local += 1
        return self.used_local - 1


class Step:
    def __init__(self, sems, moves):
        self.out, self.inn = [], []
        for src, dst, landing, dev in moves:
            k = sems.take()
            mk = functools.partial(
                pltpu.make_async_remote_copy,
                send_sem=sems.send.at[k],
                recv_sem=sems.recv.at[k],
                device_id=(dev,),
                device_id_type=pl.DeviceIdType.MESH,
            )
            self.out.append(mk(src_ref=src, dst_ref=dst))
            self.inn.append(mk(src_ref=landing, dst_ref=landing))

    def start(self):
        for m in self.out:
            m.start()

    def recv(self):
        for m in self.inn:
            m.wait_recv()

    def sent(self):
        for m in self.out:
            m.wait_send()


def gather_steps(pos, sems, g_ref, sources):
    s = pos.s
    p, q = pos.pq(pos.f, pos.g)

    def cols(lo, w):
        return (slice(None), pl.ds(lo, w))

    moves = []
    local = []
    for ref, lo, w in sources:
        k = sems.take_local()
        local.append(pltpu.make_async_copy(ref, g_ref.at[(pos.a, p, q, pos.c) + cols(lo, w)], sems.local.at[k]))
        for k in range(1, Z):
            there = g_ref.at[(pos.a, p, q, pos.c) + cols(lo, w)]
            here = g_ref.at[(pos.around_a(Z - k), p, q, pos.c) + cols(lo, w)]
            moves.append((ref, there, here, pos.dev(pos.around_a(k), pos.f, pos.g, pos.c)))
    one = Step(sems, moves)
    moves = []
    for k in range(1, s):
        pf, qf = pos.pq(pos.around_f(s - k), pos.g)
        there = g_ref.at[:, p, q, pos.c]
        moves.append((there, there, g_ref.at[:, pf, qf, pos.c], pos.dev(pos.a, pos.around_f(k), pos.g, pos.c)))
    two = Step(sems, moves)
    moves = []
    for k in range(1, s):
        for j in range(s):
            pj, qj = pos.pq(j, pos.g)
            pg, qg = pos.pq(j, pos.around_g(s - k))
            there = g_ref.at[:, pj, qj, pos.c]
            moves.append((there, there, g_ref.at[:, pg, qg, pos.c], pos.dev(pos.a, pos.f, pos.around_g(k), pos.c)))
    three = Step(sems, moves)
    there, here = g_ref.at[:, :, :, pos.c], g_ref.at[:, :, :, 1 - pos.c]
    four = Step(sems, [(there, there, here, ((pos.a * s + p) * s + q) * 2 + 1 - pos.c)])
    return local, [one, two, three, four]


class Scatter:
    def __init__(self, pos, sems, s_ref, r0, r1, r2, r3):
        self.pos, self.s_ref, self.r = pos, s_ref, (r0, r1, r2, r3)
        s, c = pos.s, pos.c
        p, q = pos.pq(pos.f, pos.g)
        steps = [Step(sems, [(s_ref.at[:, :, :, 1 - c], r0, r0, ((pos.a * s + p) * s + q) * 2 + 1 - c)])]
        moves = []
        for k in range(1, s):
            gk = pos.around_g(k)
            for j in range(s):
                pj, qj = pos.pq(j, gk)
                land = r1.at[k - 1, j]
                moves.append((s_ref.at[:, pj, qj, c], land, land, pos.dev(pos.a, pos.f, gk, c)))
        steps.append(Step(sems, moves))
        moves = []
        for k in range(1, s):
            fk = pos.around_f(k)
            pk, qk = pos.pq(fk, pos.g)
            land = r2.at[k - 1]
            moves.append((s_ref.at[:, pk, qk, c], land, land, pos.dev(pos.a, fk, pos.g, c)))
        steps.append(Step(sems, moves))
        moves = []
        for k in range(1, Z):
            ak = pos.around_a(k)
            land = r3.at[k - 1]
            moves.append((s_ref.at[ak, p, q, c], land, land, pos.dev(ak, pos.f, pos.g, c)))
        steps.append(Step(sems, moves))
        self.steps = steps

    def start(self):
        self.steps[0].start()

    def add(self, k):
        pos, s_ref = self.pos, self.s_ref
        s, c = pos.s, pos.c
        self.steps[k].recv()
        r = self.r[k]
        p, q = pos.pq(pos.f, pos.g)

        def one(at, terms):
            v = s_ref[at].astype(f32)
            for t in terms:
                v += t.astype(f32)
            s_ref[at] = v.astype(bf16)

        def slab(a, carry):
            if k == 0:
                for pp in range(s):
                    for qq in range(s):
                        one((a, pp, qq, c), [r[a, pp, qq]])
            elif k == 1:
                for j in range(s):
                    pj, qj = pos.pq(j, pos.g)
                    one((a, pj, qj, c), [r[m, j, a] for m in range(s - 1)])
            else:
                one((a, p, q, c), [r[m, a] for m in range(s - 1)])
            return carry

        lax.fori_loop(0, Z, slab, 0)
        self.steps[k + 1].start()

    def finish(self, out_ref):
        pos, r = self.pos, self.r[3]
        p, q = pos.pq(pos.f, pos.g)
        self.steps[3].recv()
        v = self.s_ref[pos.a, p, q, pos.c].astype(f32)
        for m in range(Z - 1):
            v += r[m].astype(f32)
        out_ref[...] = v
        for st in self.steps:
            st.sent()


def pieces(n):
    s = math.isqrt(n // (2 * Z))
    return [(a, p, q, c) for a in range(Z) for p in range(s) for q in range(s) for c in range(2)]


def repack(g_ref, w_ref, lo, width, n):
    at = pieces(n)
    rows = g_ref.shape[-2]
    per = math.lcm(rows, 16) // rows
    for b in range(n // per):
        for j in range(0, width, 384):
            w = min(384, width - j)
            parts = [g_ref[at[b * per + i] + (slice(None), slice(lo + j, lo + j + w))].astype(f32) for i in range(per)]
            w_ref[b * per * rows : (b + 1) * per * rows, j : j + w] = jnp.concatenate(parts, axis=0).astype(bf16)


def unpack(d_ref, s_ref, n):
    at = pieces(n)
    rows = s_ref.shape[-2]
    for k in range(n):
        s_ref[at[k]] = d_ref[k * rows : (k + 1) * rows, :].astype(bf16)


def kernel(n, grp, count_ref, tok_hbm, cot_hbm, win_hbm, wout_hbm, wup_hbm, wdn_hbm, v12_hbm, v48_hbm,
           out_hbm, tgrad_hbm, din_o, dout_o, dup_o, ddn_o,
           tok, cot, g_in, g_out, g_up, g_dn, w_in, w_out, w_up, vec, upb,
           firstT, kv_0, kv_1, mT_0, mT_1, vT_0, vT_1, p_0, p_1, cT_0, cT_1, mid_0, mid_1, n2_0, n2_1, inv_0, inv_1, sec, gl_s,
           hid, gp, dc_0, dc_1, dd_0, dd_1, ds_0, ds_1, gm_0, gm_1, acc, d_in, d_out, d_up, d_dn, d_upb,
           *rest):
    recvs, p_dn, (send_sem, recv_sem, local_sem, io_sem) = rest[:16], rest[16:-4], rest[-4:]
    images, seq, width = tok.shape
    ff = w_up.shape[1]
    heads = width // HEAD_DIM
    rp, qp = mid_0.shape[1], mT_0.shape[2]
    kv, mT, pr, cT, mid = (kv_0, kv_1), (mT_0, mT_1), (p_0, p_1), (cT_0, cT_1), (mid_0, mid_1)
    n2, inv2, vT = (n2_0, n2_1), (inv_0, inv_1), (vT_0, vT_1)
    dc, dd, ds, gm = (dc_0, dc_1), (dd_0, dd_1), (ds_0, ds_1), (gm_0, gm_1)
    live_count = count_ref[0]
    pos = Place(n)
    sems = Sems(send_sem, recv_sem, local_sem)
    whole = (ff // n) % 8 == 0
    g_dn6 = g_dn.reshape(Z, pos.s, pos.s, 2, ff // n, g_dn.shape[1]) if whole else p_dn[0]

    load_tok = pltpu.make_async_copy(tok_hbm, tok, io_sem.at[0])
    load_cot = pltpu.make_async_copy(cot_hbm, cot, io_sem.at[1])
    load_tok.start()
    load_cot.start()

    barrier = pltpu.get_barrier_semaphore()
    peers = pos.peers()
    for dev in peers:
        pl.semaphore_signal(barrier, inc=1, device_id=(dev,), device_id_type=pl.DeviceIdType.MESH)
    pl.semaphore_wait(barrier, len(peers))

    l_in, in_steps = gather_steps(pos, sems, g_in, [(win_hbm, 0, 3 * width), (v12_hbm, 3 * width, LANES)])
    l_out, out_steps = gather_steps(pos, sems, g_out, [(wout_hbm, 0, width)])
    l_up, up_steps = gather_steps(pos, sems, g_up, [(wup_hbm, 0, ff)])
    l_dn, dn_steps = gather_steps(pos, sems, g_dn6, [(wdn_hbm, 0, width), (v48_hbm, width, LANES)])
    for m in l_in + l_out + l_up + l_dn:
        m.start()
    in_steps[0].start()
    out_steps[0].start()
    for m in l_in:
        m.wait()
    in_steps[0].recv()
    in_steps[1].start()
    up_steps[0].start()
    dn_steps[0].start()
    for m in l_out:
        m.wait()
    out_steps[0].recv()
    out_steps[1].start()
    in_steps[1].recv()
    in_steps[2].start()
    out_steps[1].recv()
    out_steps[2].start()
    load_tok.wait()
    in_steps[2].recv()
    in_steps[3].start()
    out_steps[2].recv()
    out_steps[3].start()
    for m in l_up + l_dn:
        m.wait()
    for st in (up_steps, dn_steps):
        st[0].recv()
        st[1].start()
    in_steps[3].recv()
    repack(g_in, w_in, 0, w_in.shape[1], n)
    vec[...] = w_in[:, 3 * width :].astype(f32).T[:8, :]
    out_steps[3].recv()
    repack(g_out, w_out, 0, width, n)

    def row(k):
        return vec[k : k + 1, :]

    acc[...] = jnp.zeros_like(acc)
    d_in[...] = jnp.zeros_like(d_in)
    d_out[...] = jnp.zeros_like(d_out)
    d_up[...] = jnp.zeros_like(d_up)
    d_dn[...] = jnp.zeros_like(d_dn)
    d_upb[...] = jnp.zeros_like(d_upb)
    zero_head = jnp.zeros((HEAD_DIM, qp), bf16)

    def of_pair(h, v):
        return jnp.concatenate([v, zero_head] if h % 2 == 0 else [zero_head, v], axis=0)

    def head(h):
        return slice(HEAD_DIM * h, HEAD_DIM * (h + 1))

    def part(block, h):
        return slice(width * block + HEAD_DIM * h, width * block + HEAD_DIM * (h + 1))

    def pair(h, block=0):
        return slice(width * block + LANES * (h // 2), width * block + LANES * (h // 2 + 1))

    def tokens(i):
        return pad_rows(tok[i].astype(f32), rp)

    def a_first(i, b, u):
        x, _ = normalize(tokens(i))
        first = (x * row(AG) + row(AS)).astype(bf16)
        firstT[i, :width, :] = pad_rows(first, qp).T
        firstT[i, width:, :] = jnp.ones((firstT.shape[1] - width, qp), bf16)
        return first

    def a_mixed(first, b, u):
        bias = jnp.concatenate([row(QB), jnp.zeros((1, width), f32), row(VB)], axis=1)
        mixed = (nn(first, w_in[:, : 3 * width]) + bias).astype(bf16)
        kv[u][b] = mixed[:, width:]
        turned = pad_rows(mixed, qp).T
        mT[u][b] = turned[: 2 * width, :]
        vT[u][...] = turned[2 * width :, :]

    def a_probs(b, u):
        key_row = lax.broadcasted_iota(jnp.int32, (rp, qp), 0)
        for h in range(heads):
            s = nn(kv[u][b, :, pair(h)], of_pair(h, mT[u][b, part(0, h), :]))
            e = jnp.where(key_row < seq, jnp.exp2(s * (SCALE * LOG2E)), 0.0)
            pr[u][b, h] = (e * (1.0 / jnp.sum(e, axis=0, keepdims=True))).astype(bf16)

    def a_context(b, u):
        for h in range(heads):
            cT[u][b, head(h), :] = nn(vT[u][head(h), :rp], pr[u][b, h]).astype(bf16)

    def a_middle(i, b, u):
        mid[u][b] = tokens(i) + tn(cT[u][b], w_out[...])[:rp] + row(OB)

    def gather_tick(t):
        for k, (last, nxt) in enumerate(((1, 2), (2, 3))):
            @pl.when(t == 1 + 2 * k)
            def _():
                for st in (up_steps, dn_steps):
                    st[last].recv()
                    st[nxt].start()

    def a_body(i, b, u, i1, b1, u1, i2, b2, u2):
        first = a_first(i, b, u)
        a_probs(b1, u1)
        a_mixed(first, b, u)
        if i2 is not None:
            a_middle(i2, b2, u2)
        a_context(b1, u1)

    a_mixed(a_first(0, 0, 0), 0, 0)
    a_body(1, 0, 1, 0, 0, 0, None, None, None)

    def a_pair(t, carry):
        gather_tick(t)
        i = 2 * t + 2
        a_body(i, t + 1, 0, i - 1, t, 1, i - 2, t, 0)
        a_body(i + 1, t + 1, 1, i, t + 1, 0, i - 1, t, 1)
        return carry

    half = images // 2
    lax.fori_loop(0, half - 1, a_pair, 0)
    a_probs(half - 1, 1)
    a_middle(images - 2, half - 1, 0)
    a_context(half - 1, 1)
    a_middle(images - 1, half - 1, 1)

    for st in (up_steps, dn_steps):
        st[3].recv()
    repack(g_up, w_up, 0, ff, n)
    if not whole:
        repack(g_dn6, g_dn, 0, g_dn.shape[1], n)
    upb[...] = g_dn[:, width:].astype(f32).T[:8, :]
    load_cot.wait()
    for steps in (in_steps, out_steps, up_steps, dn_steps):
        for st in steps:
            st.sent()

    def rows(k):
        return pl.ds(pl.multiple_of(k * rp, 16), rp)

    def b_norm(i, b, u, k):
        n2[u][...], inv2[u][...] = normalize(mid[u][b])
        sec[rows(k), :] = (n2[u][...] * row(FG) + row(FS)).astype(bf16)
        gl_s[rows(k), :] = jnp.where(i < live_count, pad_rows(cot[i].astype(f32), rp), 0.0).astype(bf16)

    def b_hidden(k):
        second, grad = sec[rows(k), :], gl_s[rows(k), :]
        for j in range(ff // 256):
            cols = slice(256 * j, 256 * (j + 1))
            v = nn(second, w_up[:, cols]) + upb[0:1, cols]
            gh = nt(grad, g_dn[cols, :width])
            phi = 0.5 + 0.5 * lax.erf(v * math.sqrt(0.5))
            dens = jnp.exp2(v * v * (-0.5 * LOG2E))
            hid[rows(k), cols] = (v * phi).astype(bf16)
            gp[rows(k), cols] = (gh * (phi + v * dens * (1 / math.sqrt(2 * math.pi)))).astype(bf16)

    def b_out(i, b, u, k):
        y = nn(hid[rows(k), :], g_dn[:, :width]) + mid[u][b] + row(DB)
        cot[i] = jnp.where(i < live_count, y, 0.0).astype(bf16)[:seq]

    def b_back(b, u, k):
        gs = nt(gp[rows(k), :], w_up[...])
        grad, normed = gl_s[rows(k), :].astype(f32), n2[u][...]
        gmid = grad + norm_back(gs * row(FG), normed, inv2[u][...])
        mid[u][b] = gmid
        acc[8 * DB : 8 * DB + 8, :] += fold8(grad)
        acc[8 * FG : 8 * FG + 8, :] += fold8(gs * normed)
        acc[8 * FS : 8 * FS + 8, :] += fold8(gs)
        acc[8 * OB : 8 * OB + 8, :] += fold8(gmid.astype(bf16).astype(f32))

    def b_outw(b, u):
        d_out[...] += nn(cT[u][b][:, :rp], mid[u][b].astype(bf16))

    def b_body(i, b, u, b1, u1, k):
        b_out(i - 1, b1, u1, k - 1)
        b_back(b1, u1, k - 1)
        b_norm(i, b, u, k)
        b_hidden(k)
        b_outw(b1, u1)

    def b_group(t, carry):
        i0, b0 = t * grp, t * (grp // 2)
        b_norm(i0, b0, 0, 0)
        b_hidden(0)

        def b_pair(r, c):
            i = i0 + 2 * r + 1
            b_body(i, b0 + r, 1, b0 + r, 0, 2 * r + 1)
            b_body(i + 1, b0 + r + 1, 0, b0 + r, 1, 2 * r + 2)
            return c

        lax.fori_loop(0, grp // 2 - 1, b_pair, 0)
        be = b0 + grp // 2 - 1
        b_body(i0 + grp - 1, be, 1, be, 0, grp - 1)
        b_out(i0 + grp - 1, be, 1, grp - 1)
        b_back(be, 1, grp - 1)
        b_outw(be, 1)

        def b_weights(j, c):
            cols = pl.ds(pl.multiple_of(j * 512, 512), 512)
            d_up[:, cols] += tn(sec[...], gp[:, cols])
            d_dn[:, cols] += tn(gl_s[...], hid[:, cols])
            d_upb[:, cols] += nn(jnp.ones((d_upb.shape[0], gp.shape[0]), bf16), gp[:, cols])
            return c

        lax.fori_loop(0, ff // 512, b_weights, 0)
        return carry

    lax.fori_loop(0, images // grp, b_group, 0)
    store_out = pltpu.make_async_copy(cot, out_hbm, io_sem.at[1])
    store_out.start()

    rs_in, rs_out, rs_up, rs_dn = [
        Scatter(pos, sems, ref, *recvs[4 * k : 4 * k + 4]) for k, ref in enumerate((g_in, g_out, g_up, g_dn6))
    ]
    unpack(d_up, g_up, n)
    rs_up.start()
    for j in range(0, ff, LANES):
        block = jnp.concatenate([d_dn[:, j : j + LANES], pad_rows(d_upb[:8, j : j + LANES], LANES)], axis=0)
        g_dn[j : j + LANES, :] = block.T.astype(bf16)
    if not whole:
        unpack(g_dn, g_dn6, n)
    rs_dn.start()
    unpack(d_out, g_out, n)
    rs_out.start()
    early = (rs_up, rs_dn, rs_out)

    def c_context(b, u):
        g = nt(w_out[...], pad_rows(mid[u][b].astype(bf16), qp)).astype(bf16)
        dc[u][...] = g
        prod = g.astype(f32) * cT[u][b].astype(f32)
        sums = [jnp.sum(prod[head(h), :], axis=0, keepdims=True) for h in range(heads)]
        dd[u][...] = jnp.concatenate(sums + [jnp.zeros((8 - heads, qp), f32)], axis=0)

    def c_scores(b, u):
        for h in range(heads):
            dp = nn(kv[u][b, :, pair(h, 1)], of_pair(h, dc[u][head(h), :]))
            ds[u][h] = (pr[u][b, h].astype(f32) * (dp - dd[u][h : h + 1, :])).astype(bf16)

    def c_value(b, u):
        for h in range(heads):
            gm[u][part(2, h), :rp] = nt(dc[u][head(h), :], pr[u][b, h]).astype(bf16)

    def c_query_key(b, u):
        for h in range(heads):
            g = ds[u][h]
            gm[u][part(0, h), :] = (nn(mT[u][b, part(1, h), :rp], g) * SCALE).astype(bf16)
            gm[u][part(1, h), :rp] = (nt(mT[u][b, part(0, h), :], g) * SCALE).astype(bf16)

    def c_inw(i, u):
        d_in[:, : 3 * width] += nt(firstT[i][:, :rp], gm[u][:, :rp])

    def c_first(i, b, u):
        gf = nn(w_in[:, : 3 * width], gm[u][...]).T[:rp]
        normed, inv = normalize(tokens(i))
        acc[8 * AG : 8 * AG + 8, :] += fold8(gf * normed)
        acc[8 * AS : 8 * AS + 8, :] += fold8(gf)
        tok[i] = (mid[u][b] + norm_back(gf * row(AG), normed, inv)).astype(bf16)[:seq]

    def scatter_tick(t):
        for k in range(3):
            @pl.when(t == 1 + k)
            def _():
                for rs in early:
                    rs.add(k)

    def c_body(b, u, b1, u1, i2, b2, u2):
        if i2 is not None:
            c_inw(i2, u2)
        c_scores(b1, u1)
        if i2 is not None:
            c_first(i2, b2, u2)
        c_value(b1, u1)
        if b is not None:
            c_context(b, u)
        c_query_key(b1, u1)

    c_context(0, 0)
    c_body(0, 1, 0, 0, None, None, None)

    def c_pair(t, carry):
        scatter_tick(t)
        i = 2 * t + 2
        c_body(t + 1, 0, t, 1, i - 2, t, 0)
        c_body(t + 1, 1, t + 1, 0, i - 1, t, 1)
        return carry

    lax.fori_loop(0, half - 1, c_pair, 0)
    c_body(None, None, half - 1, 1, images - 2, half - 1, 0)
    c_inw(images - 1, 1)
    sums = {QB: d_in[width : width + 1, :width], VB: d_in[width : width + 1, 2 * width : 3 * width]}

    def c_vectors():
        table = []
        for k in range(8):
            table.append(sums[k] if k in sums else jnp.sum(acc[8 * k : 8 * k + 8, :], axis=0, keepdims=True))
        d_in[:width, 3 * width :] = pad_rows(jnp.concatenate(table, axis=0), LANES).T

    c_first(images - 1, half - 1, 1)
    store_tgrad = pltpu.make_async_copy(tok, tgrad_hbm, io_sem.at[0])
    store_tgrad.start()
    c_vectors()
    unpack(d_in, g_in, n)
    rs_in.start()
    rs_up.finish(dup_o)
    rs_dn.finish(ddn_o)
    rs_out.finish(dout_o)
    for k in range(3):
        rs_in.add(k)
    rs_in.finish(din_o)
    store_out.wait()
    store_tgrad.wait()


def build(n, images, seq, width, ff):
    heads = width // HEAD_DIM
    rp, qp = -(-seq // 16) * 16, -(-seq // LANES) * LANES
    s = math.isqrt(n // (2 * Z))
    grp = 6 if n <= 32 else 2
    half = images // 2
    rows, rows_ff = width // n, ff // n

    def vm(*shape, dtype=bf16):
        return pltpu.VMEM(shape, dtype)

    def twice(*shape, dtype=bf16):
        return [vm(*shape, dtype=dtype)] * 2

    lead = (Z, s, s, 2)
    chunks = ((rows, 3 * width + LANES), (rows, width), (rows, ff), (rows_ff, width + LANES))
    recvs = []
    for rc in chunks:
        recvs += [vm(Z, s, s, *rc), vm(s - 1, s, Z, *rc), vm(s - 1, Z, *rc), vm(Z - 1, *rc)]
    remote = 2 * 4 * (Z - 1 + (s - 1) + (s - 1) * s + 1) + 2 * (Z - 1)
    scratch = [
        vm(images, seq, width),
        vm(images, seq, width),
        vm(*lead, *chunks[0]),
        vm(*lead, *chunks[1]),
        vm(*lead, *chunks[2]),
        vm(ff, width + LANES),
        vm(width, 3 * width + LANES),
        vm(width, width),
        vm(width, ff),
        vm(8, width, dtype=f32),
        vm(8, ff, dtype=f32),
        vm(images, width + 16, qp),
        *twice(half, rp, 2 * width),
        *twice(half, 2 * width, qp),
        *twice(width, qp),
        *twice(half, heads, rp, qp),
        *twice(half, width, qp),
        *twice(half, rp, width, dtype=f32),
        *twice(rp, width, dtype=f32),
        *twice(rp, 1, dtype=f32),
        vm(grp * rp, width),
        vm(grp * rp, width),
        vm(grp * rp, ff),
        vm(grp * rp, ff),
        *twice(width, qp),
        *twice(8, qp, dtype=f32),
        *twice(heads, rp, qp),
        *twice(3 * width, qp),
        vm(64, width, dtype=f32),
        vm(width + 16, 3 * width + LANES, dtype=f32),
        vm(width, width, dtype=f32),
        vm(width, ff, dtype=f32),
        vm(width, ff, dtype=f32),
        vm(16, ff, dtype=f32),
        *recvs,
        *([] if rows_ff % 8 == 0 else [vm(*lead, *chunks[3])]),
        pltpu.SemaphoreType.DMA((remote,)),
        pltpu.SemaphoreType.DMA((remote,)),
        pltpu.SemaphoreType.DMA((6,)),
        pltpu.SemaphoreType.DMA((2,)),
    ]
    anywhere = pl.BlockSpec(memory_space=pl.ANY)
    vmem = pl.BlockSpec(memory_space=pltpu.VMEM)
    shape = jax.ShapeDtypeStruct
    return pl.pallas_call(
        functools.partial(kernel, n, grp),
        in_specs=[pl.BlockSpec(memory_space=pltpu.SMEM)] + [anywhere] * 8,
        out_specs=[anywhere] * 2 + [vmem] * 4,
        out_shape=[shape((images, seq, width), bf16)] * 2 + [shape(rc, f32) for rc in chunks],
        scratch_shapes=scratch,
        compiler_params=pltpu.CompilerParams(
            collective_id=0, has_side_effects=True, vmem_limit_bytes=67043328
        ),
        name="encoder",
    )


def shards(
    tokens, cotangent, image_count, attention_gain, attention_shift, input_weight, query_bias, value_bias,
    output_weight, output_bias, feed_gain, feed_shift, up_weight, up_bias, down_weight, down_bias, *, n,
):
    images, seq, width = tokens.shape
    ff = up_weight.shape[1]
    vectors = (attention_gain, attention_shift, query_bias, value_bias, output_bias, feed_gain, feed_shift, down_bias)
    v12 = jnp.pad(jnp.stack(vectors, axis=1), ((0, 0), (0, LANES - 8)))
    v48 = jnp.pad(up_bias[:, None], ((0, 0), (0, LANES - 1)))
    out, tgrad, d_in, d_out, d_up, d_dn = build(n, images, seq, width, ff)(
        image_count, tokens, cotangent, input_weight, output_weight, up_weight, down_weight, v12, v48
    )
    col = [d_in[:, 3 * width + k] for k in range(8)]
    return (
        out, tgrad, col[AG], col[AS], d_in[:, : 3 * width], col[QB], col[VB], d_out, col[OB], col[FG], col[FS],
        d_up, d_dn[:, width], d_dn[:, :width], col[DB],
    )


def solution(mesh):
    n = mesh.shape["shard"]
    cube, flat, mat = P("shard", None, None), P("shard"), P("shard", None)
    return jax.shard_map(
        functools.partial(shards, n=n),
        mesh=mesh,
        in_specs=(cube, cube, flat, flat, flat, mat, flat, flat, mat, flat, flat, flat, mat, flat, mat, flat),
        out_specs=(cube, cube, flat, flat, mat, flat, flat, mat, flat, flat, flat, mat, flat, mat, flat),
        check_vma=False,
    )
```

time: 743 us -> 150 us (0.20)
  blocking collectives: 244 us -> 0 us
  matrix products: 176 us -> 0 us
  Pallas kernels: 0 us -> 128 us
  local copies, waits for them, and re-layouts: 145 us -> 19.9 us
  other arithmetic: 74.5 us -> 0 us
  starting transfers between devices: 65.5 us -> 0 us
  between operations: 14.7 us -> 1.32 us
  loops' own time: 10.8 us -> 0 us
    dot_general x54 -> x0, matrix products: 176 us -> none  [the longest x3 42.2 us: feed_forward(): jnp.dot(input_b, up_weight, preferred_element_type=jnp.float32) + up_bias]
    unnamed x3 -> x0, blocking collectives: 159 us -> none
    pallas_call x0 -> x1, Pallas kernels: none -> 128 us  [shards(): build(n, images, seq, width, ff)]
    all_gather x2 -> x0, blocking collectives: 85 us -> none  [the longest x1 47.1 us: shards(): lax.all_gather(input_weight, 'shard', axis=0, tiled=True)]
    unnamed x24 -> x0, starting transfers between devices: 65.4 us -> none
    reshape x24 -> x0, local copies, waits for them, and re-layouts: 38.5 us -> none  [the longest x6 15.1 us: attention_backward(): grad_context.astype(jnp.bfloat16)]
    convert_element_type x12 -> x0, local copies, waits for them, and re-layouts: 32.2 us -> none  [the longest x6 27.3 us: attention_backward(): jnp.stack([grad_query, grad_key, grad_value], axis=2).astype(jnp.bfloat16)]
    add x27 -> x0, other arithmetic: 31.8 us -> none  [whole_step(): grad_total = jax.tree.map(jnp.add, grad_total, grad_parts)]
  transfers between devices with their start and end apart: 27 -> 0, of which waited for: 2 -> 0; matrix products, arithmetic and copies ran while one was open for 14% -> 0% of each run, Pallas kernels for 0% -> 0%
where the time goes in v1:
time: 150 us; the launch traced here: 149 us
  Pallas kernels  128 us (85%)
  local copies, waits for them, and re-layouts  19.9 us (13%)
    pallas_call x1, Pallas kernels, shards(): build(n, images, seq, width, ff)  128 us
    another operation x9, local copies, waits for them, and re-layouts, shards(): v12 = jnp.pad(jnp.stack(vectors, axis=1), ((0, 0), (0, LANES - 8)))  6.14 us
    unnamed x10, local copies, waits for them, and re-layouts  5.54 us

profile of v1, /device:TPU:0, one launch (start us, length us, event | category | flops | bytes accessed | tf_op | source)
XLA Modules:
  0.0 149.1 jit_solution(10429363257695443913)
XLA Ops:
  0.6 0.7 copy.40
  1.4 0.8 copy.41
  2.1 0.8 copy.42
  2.9 0.8 copy.43
  3.7 0.8 copy.44
  4.4 0.8 copy.45
  5.2 0.8 copy.46
  5.9 0.8 copy.47
  6.7 0.1 stack.35
  6.8 0.6 pad.8.v12_hbm
  7.4 0.8 copy.48
  8.2 0.6 pad.9.v48_hbm
  9.4 127.9 %encoder.1 = (bf16[12,197,384]{2,1,0:T(8,128)(2,1)}, bf16[12,197,384]{2,1,0:T(8,128)(2,1)}, f32[12,1280]{1,0:T(8,128)}, f32[12,384]{1,0:T(8,128)}, f32[12,1536]{1,0:T(8,128)}, /*index=5*/f32[48,512]{1,0:T(8,128)}) custom-call(s32[1]{0:T(128)S(6)} %copy.53.count_ref, bf16[12,197,384]{2,1,0:T(8,128)(2,1)} %tok_hbm.1, bf16[12,197,384]{2,1,0:T(8,128)(2,1)} %cot_hbm.1, ...), custom_call_target="tpu_custom_call" | custom-call | tf_op jit(solution)/shard_map/encoder/pallas_call | solution.py:695
  137.3 1.8 %slice_reduce_fusion.1 = (f32[12]{0:T(128)}, f32[12]{0:T(128)}, f32[12]{0:T(128)}, f32[12]{0:T(128)}, f32[12]{0:T(128)}, /*index=5*/f32[12]{0:T(128)}, f32[12]{0:T(128)}, f32[12]{0:T(128)}) fusion(f32[12,1280]{1,0:T(8,128)} %get-tuple-element.23), kind=kLoop, calls=%fused_computation.1 | loop fusion | bytes 768 | tf_op jit(solution)/shard_map/slice | solution.py:698
  139.1 1.5 %slice.35 = f32[12,1152]{1,0:T(8,128)} slice(f32[12,1280]{1,0:T(8,128)} %get-tuple-element.23), slice={[0:12], [0:1152]} | slice | bytes 110592 | tf_op jit(solution)/shard_map/slice | solution.py:700
  140.7 1.5 %slice.42 = f32[48,384]{1,0:T(8,128)} slice(f32[48,512]{1,0:T(8,128)} %get-tuple-element.26), slice={[0:48], [0:384]} | slice | bytes 147456 | tf_op jit(solution)/shard_map/slice | solution.py:701
  142.2 1.4 slice_reduce_fusion
  143.5 0.0 copy-start
  143.5 3.1 %copy.54 = bf16[12,197,384]{2,1,0:T(8,128)(2,1)} copy(bf16[12,197,384]{2,1,0:T(8,128)(2,1)} %get-tuple-element.50) | data formatting | bytes 3631104
  146.6 0.0 copy-done
  146.6 0.0 copy-start.2
  146.6 0.0 copy-start.1
  146.6 1.2 copy.55
  147.8 0.0 copy-done.2
  147.8 0.6 copy.56
  148.4 0.0 copy-done.1
  148.4 0.6 copy.57
Async XLA Ops:
  143.5 3.1 %copy-start = (bf16[12,197,384]{2,1,0:T(8,128)(2,1)S(1)}, bf16[12,197,384]{2,1,0:T(8,128)(2,1)}, u32[]{:S(2)}) copy-start(bf16[12,197,384]{2,1,0:T(8,128)(2,1)} %get-tuple-element.51) | copy-start | bytes 5446660
  146.6 1.2 copy-start.2
  146.6 1.8 %copy-start.1 = (f32[12,1536]{1,0:T(8,128)S(1)}, f32[12,1536]{1,0:T(8,128)}, u32[]{:S(2)}) copy-start(f32[12,1536]{1,0:T(8,128)} %get-tuple-element.61) | copy-start | bytes 221188
